TPU v7x, 32 devices: a whole 2x2x4 slice. The times are simulated.
32 devices in a mesh: gx: 4 (over x, core), gy: 4 (over z), gz: 2 (over y).
Axes of the slice: x: 2, y: 2, z: 4, core: 2. Of those that a mesh axis runs over, the one named last changes fastest.
Arguments:
- deflation: bfloat16 [32, 16, 8, 3, 128], P('gx', 'gy', 'gz'), may hold values from -0.33 to 0.33
- material: int32 [32, 16, 8], P('gx', 'gy', 'gz'), may hold values from 0 to 15
- moduli: float32 [16], replicated, may hold values from 1 to 100
- stencil: float32 [27, 3, 3], replicated, may hold values from -0.6 to 0.6
Outputs:
- coarse: float32 [4, 4, 128, 2, 27, 128], P('gx', 'gy', 'gz')
All inputs are finite; a program needn't handle non-finite values.
Results may differ from a plain program's by a relative error of at most 0.005.
Values may be sent and summed in bfloat16 or wider, within the bound.
No kernel may reach another device: no remote copies, remote signals or barrier semaphores. Data moves between devices by JAX's collectives and lax.ppermute only.
A program may use at most 64 MiB of HBM per device.

v0:
```python
import functools

import jax
import jax.numpy as jnp
from jax import lax
from jax.experimental import pallas as pl
from jax.experimental.pallas import tpu as pltpu
from jax.sharding import PartitionSpec as P

VMEM = pltpu.VMEM
LANES = 128


def scale_kernel(classes, moduli_ref, material_ref, vectors_ref, out_ref):
    cells_y, cells_z, cells_x = material_ref.shape
    parts = vectors_ref.shape[2]
    roots = []
    for y in range(cells_y):
        material = material_ref[y]
        modulus = jnp.zeros(material.shape, jnp.float32)
        for c in range(classes):
            modulus = jnp.where(material == c, moduli_ref[c], modulus)
        roots.append(jnp.sqrt(modulus))
    for x in range(cells_x):
        for y in range(cells_y):
            factor = jnp.broadcast_to(roots[y][:, x : x + 1], (cells_z, vectors_ref.shape[-1]))
            for a in range(parts):
                row = (y * parts + a) * cells_z
                value = vectors_ref[x, y, a].astype(jnp.float32) * factor
                out_ref[x, row : row + cells_z, :] = value.astype(jnp.bfloat16)


def weight_kernel(cells_y, cells_z, table_ref, out_ref):
    count, rows, lanes = out_ref.shape
    half = rows // 2
    table = table_ref[...]
    high = table.astype(jnp.bfloat16)
    low = (table - high.astype(jnp.float32)).astype(jnp.bfloat16)
    row = lax.broadcasted_iota(jnp.int32, (rows, lanes), 0)
    row = jnp.where(row >= half, row - half, row)
    lane = lax.broadcasted_iota(jnp.int32, (rows, lanes), 1)
    block = 3 * cells_z
    row_y, row_z = row // block, row % cells_z
    slot, lane_z = lane // block, lane % cells_z
    lane_y = jnp.where(slot < cells_y, slot, jnp.where(slot == cells_y, -1, cells_y))
    inside = slot < cells_y + 2
    shift_y = lane_y - row_y
    pick_row = lax.broadcasted_iota(jnp.int32, (half, table.shape[0]), 0)
    pick_col = lax.broadcasted_iota(jnp.int32, (half, table.shape[0]), 1)
    part = (pick_row % block) // cells_z
    spread_row = lax.broadcasted_iota(jnp.int32, (table.shape[1], lanes), 0)
    spread_lane = lax.broadcasted_iota(jnp.int32, (table.shape[1], lanes), 1)
    lane_part = (spread_lane % block) // cells_z
    for k in range(3):
        spread = (spread_row == 3 * k + lane_part).astype(jnp.float32).astype(jnp.bfloat16)
        totals = [jnp.zeros((rows, lanes), jnp.float32) for _ in range(3)]
        wide_high = jnp.dot(high, spread, preferred_element_type=jnp.float32).astype(jnp.bfloat16)
        wide_low = jnp.dot(low, spread, preferred_element_type=jnp.float32).astype(jnp.bfloat16)
        for dy in range(3):
            for dz in range(3):
                pick = (pick_col == 9 * part + 3 * dy + dz).astype(jnp.float32).astype(jnp.bfloat16)
                value = jnp.concatenate(
                    [
                        jnp.dot(pick, wide_high, preferred_element_type=jnp.float32),
                        jnp.dot(pick, wide_low, preferred_element_type=jnp.float32),
                    ],
                    axis=0,
                )
                on_y = inside & (shift_y == dy - 1)
                for oz in range(3):
                    shift_z = lane_z + (oz - 1) * cells_z - row_z
                    totals[oz] = jnp.where(on_y & (shift_z == dz - 1), value, totals[oz])
        for oz in range(3):
            out_ref[3 * k + oz] = totals[oz].astype(jnp.bfloat16)


def block_kernel(sizes, weights_ref, field_ref, out_ref, turned_ref, image_ref):
    cells_x, own_rows, rows, owners, share, me = sizes
    width = field_ref.shape[-1]
    first = lax.axis_index("gz") * share
    lane = lax.broadcasted_iota(jnp.int32, (share, LANES), 1)
    side = own_rows // 4
    masks = [
        (lane >= own_rows) & (lane < own_rows + side),
        lane < own_rows,
        (lane >= own_rows + side) & (lane < rows),
    ]
    pad = jnp.zeros((LANES - rows, width), jnp.bfloat16)
    stride = 27 * owners

    def plane(v, x):
        return jnp.concatenate([field_ref[v, x], pad], axis=0)

    for u in range(owners):
        for x in range(cells_x):
            own = field_ref[u, x, 0:own_rows, :]
            turned_ref[...] = jnp.concatenate([own, own], axis=0).T
            image_ref[x * share : (x + 1) * share, :] = turned_ref[pl.ds(first, share), :]
        lhs = image_ref[...]
        for oz in range(3):
            v = u + oz - 1
            if v < 0 or v >= owners:
                zero = jnp.zeros((share, width), jnp.float32)
                for n in range(oz, 27, 3):
                    out_ref[pl.ds(n * owners + u, share, stride=stride), :] = zero
                continue
            products = [
                jnp.dot(lhs, weights_ref[3 * k + oz], preferred_element_type=jnp.float32) for k in range(3)
            ]

            def image(x):
                total = None
                for k in range(3):
                    source = x - (k - 1)
                    if 0 <= source < cells_x:
                        term = products[k][source * share : (source + 1) * share, :]
                        total = term if total is None else total + term
                return jnp.concatenate(
                    [jnp.where(mask, total, 0.0).astype(jnp.bfloat16) for mask in masks], axis=0
                )

            middle = None
            for x in range(0, cells_x, 2):
                left = jnp.concatenate([image(x), image(x + 1)], axis=1)
                right = jnp.concatenate([plane(v, x), plane(v, x + 1)], axis=0)
                term = jnp.dot(left, right, preferred_element_type=jnp.float32)
                middle = term if middle is None else middle + term
            before = jnp.dot(image(-1), plane(v, cells_x), preferred_element_type=jnp.float32)
            after = jnp.dot(image(cells_x), plane(v, cells_x + 1), preferred_element_type=jnp.float32)
            for ox, value in enumerate((before, middle, after)):
                for oy in range(3):
                    n = 9 * ox + 3 * oy + oz
                    out_ref[pl.ds(n * owners + u, share, stride=stride), :] = value[
                        oy * share : (oy + 1) * share, :
                    ]


def cyclic(array, axis, step):
    peers = lax.axis_size(axis)
    return lax.ppermute(array, axis, [(i, (i + step) % peers) for i in range(peers)])


def halo(first, last, axis):
    peers, place = lax.axis_size(axis), lax.axis_index(axis)
    before = cyclic(last, axis, 1)
    after = cyclic(first, axis, -1)
    zero = jnp.zeros_like(before)
    return jnp.where(place == 0, zero, before), jnp.where(place == peers - 1, zero, after)


def body(deflation, material, moduli, stencil):
    cells_x, cells_y, cells_z, parts, width = deflation.shape
    owners = lax.axis_size("gz")
    share = width // owners
    side = parts * cells_z
    own_rows = cells_y * side
    rows = own_rows + 2 * side
    small = pltpu.CompilerParams(vmem_limit_bytes=16 << 20)

    scaled = pl.pallas_call(
        functools.partial(scale_kernel, moduli.shape[0]),
        out_shape=jax.ShapeDtypeStruct((cells_x, own_rows, width), jnp.bfloat16),
        in_specs=[
            pl.BlockSpec(memory_space=pltpu.SMEM),
            pl.BlockSpec(memory_space=VMEM),
            pl.BlockSpec(memory_space=VMEM),
        ],
        out_specs=pl.BlockSpec(memory_space=VMEM),
        compiler_params=small,
        name="scale",
    )(moduli, jnp.transpose(material, (1, 2, 0)), jnp.transpose(deflation, (0, 1, 3, 2, 4)))

    before, after = halo(scaled[:, :side], scaled[:, own_rows - side :], "gy")
    planes = jnp.concatenate([scaled, before, after], axis=1)
    left, right = halo(planes[0:1], planes[cells_x - 1 :], "gx")
    field = jnp.concatenate([planes, left, right], axis=0)
    if owners == 2:
        other = cyclic(field, "gz", 1)
        lines = jnp.where(lax.axis_index("gz") == 0, jnp.stack([field, other]), jnp.stack([other, field]))
    else:
        lines = lax.all_gather(field, "gz")

    table = jnp.transpose(stencil.reshape(3, 9, 3, 3), (2, 1, 0, 3)).reshape(27, 9)
    weights = pl.pallas_call(
        functools.partial(weight_kernel, cells_y, cells_z),
        out_shape=jax.ShapeDtypeStruct((9, 2 * own_rows, LANES), jnp.bfloat16),
        in_specs=[pl.BlockSpec(memory_space=VMEM)],
        out_specs=pl.BlockSpec(memory_space=VMEM),
        compiler_params=small,
        name="weights",
    )(table)

    sizes = (cells_x, own_rows, rows, owners, share, None)
    coarse = pl.pallas_call(
        functools.partial(block_kernel, sizes),
        out_shape=jax.ShapeDtypeStruct((share * 27 * owners, width), jnp.float32),
        in_specs=[pl.BlockSpec(memory_space=VMEM)] * 2,
        out_specs=pl.BlockSpec(memory_space=VMEM),
        scratch_shapes=[
            VMEM((width, 2 * own_rows), jnp.bfloat16),
            VMEM((cells_x * share, 2 * own_rows), jnp.bfloat16),
        ],
        compiler_params=pltpu.CompilerParams(vmem_limit_bytes=32 << 20),
        name="blocks",
    )(weights, lines)
    coarse = coarse.reshape(share, 27, owners, width)
    return jnp.transpose(coarse, (0, 2, 1, 3)).reshape(1, 1, share, owners, 27, width)


def solution(mesh):
    in_specs = (P("gx", "gy", "gz", None, None), P("gx", "gy", "gz"), P(), P())
    out_specs = P("gx", "gy", "gz", None, None, None)
    return jax.shard_map(body, mesh=mesh, in_specs=in_specs, out_specs=out_specs, check_vma=False)
```

profile of v0, /device:TPU:0, one launch (start us, length us, event | category | flops | bytes accessed | tf_op | source)
XLA Modules:
  0.0 23.5 jit_solution(15273952660899990202)
XLA Ops:
  0.0 0.0 copy-start
  0.0 0.9 %copy-done = bf16[8,4,4,3,128]{4,2,3,1,0:T(4,128)(2,1)S(1)} copy-done((bf16[8,4,4,3,128]{4,2,3,1,0:T(4,128)(2,1)S(1)}, bf16[8,4,4,3,128]{4,2,3,1,0:T(4,128)(2,1)}, u32[]{:S(2)}) %copy-start) | copy-done | bytes 98328
  0.9 0.0 copy-start.1
  0.9 0.7 %copy-done.1 = s32[8,4,4]{0,2,1:T(4,128)S(1)} copy-done((s32[8,4,4]{0,2,1:T(4,128)S(1)}, s32[8,4,4]{0,2,1:T(4,128)}, u32[]{:S(2)}) %copy-start.1) | copy-done | bytes 536
  1.6 0.0 copy-start.2
  1.6 0.7 %copy-done.2 = f32[16]{0:T(128)S(1)} copy-done((f32[16]{0:T(128)S(1)}, f32[16]{0:T(128)}, u32[]{:S(2)}) %copy-start.2) | copy-done | bytes 88
  2.2 0.7 %scale.1 = bf16[8,48,128]{2,1,0:T(8,128)(2,1)S(1)} custom-call(f32[16]{0:T(128)S(1)} %copy-done.2, s32[4,4,8]{2,1,0:T(4,128)S(1)} %bitcast.18, bf16[8,4,3,4,128]{4,3,2,1,0:T(4,128)(2,1)S(1)} %bitcast.17), custom_call_target="tpu_custom_call" | custom-call | tf_op jit(solution)/shard_map/scale/pallas_call | solution.py:160
  3.0 3.1 %collective-permute-start = (bf16[8,12,128]{2,1,0:T(8,128)(2,1)S(1)}, bf16[8,12,128]{2,1,0:T(8,128)(2,1)S(1)}, u32[]{:S(2)}, u32[]{:S(2)}) collective-permute-start(bf16[8,12,128]{2,1,0:T(8,128)(2,1)S(1)} %get-tuple-element.7), channel_id=1, source_target_pairs={{0,2},{2,4},{4,6},{6,0},{1,3},{3,5},{5,7},{7,1},{8,10},{10,12},{12... | collective-permute-start | bytes 73736 | tf_op jit(solution)/shard_map/ppermute | solution.py:140
  6.1 2.1 %collective-permute-start.1 = (bf16[8,12,128]{2,1,0:T(8,128)(2,1)S(1)}, bf16[8,12,128]{2,1,0:T(8,128)(2,1)S(1)}, u32[]{:S(2)}, u32[]{:S(2)}) collective-permute-start(bf16[8,12,128]{2,1,0:T(8,128)(2,1)S(1)} %get-tuple-element.8), channel_id=1, source_target_pairs={{0,6},{2,0},{4,2},{6,4},{1,7},{3,1},{5,3},{7,5},{8,14},{10,8},{12,... | collective-permute-start | bytes 73736 | tf_op jit(solution)/shard_map/ppermute | solution.py:140
  8.1 1.9 %collective-permute-done = bf16[8,12,128]{2,1,0:T(8,128)(2,1)S(1)} collective-permute-done((bf16[8,12,128]{2,1,0:T(8,128)(2,1)S(1)}, bf16[8,12,128]{2,1,0:T(8,128)(2,1)S(1)}, u32[]{:S(2)}, u32[]{:S(2)}) %collective-permute-start) | collective-permute-done | bytes 24608 | tf_op jit(solution)/shard_map/ppermute | solution.py:140
  10.1 0.2 %collective-permute-done.1 = bf16[8,12,128]{2,1,0:T(8,128)(2,1)S(1)} collective-permute-done((bf16[8,12,128]{2,1,0:T(8,128)(2,1)S(1)}, bf16[8,12,128]{2,1,0:T(8,128)(2,1)S(1)}, u32[]{:S(2)}, u32[]{:S(2)}) %collective-permute-start.1) | collective-permute-done | bytes 24608 | tf_op jit(solution)/shard_map/ppermute | solution.py:140
  10.3 0.1 collective-permute-start.2
  10.4 1.7 %collective-permute-start.3 = (bf16[1,72,128]{2,1,0:T(8,128)(2,1)S(1)}, bf16[1,72,128]{2,1,0:T(8,128)(2,1)S(1)}, u32[]{:S(2)}, u32[]{:S(2)}) collective-permute-start(bf16[1,72,128]{2,1,0:T(8,128)(2,1)S(1)} %get-tuple-element.6), channel_id=1, source_target_pairs={{0,24},{8,0},{16,8},{24,16},{1,25},{9,1},{17,9},{25,17},{2,26},{10... | collective-permute-start | bytes 55304 | tf_op jit(solution)/shard_map/ppermute | solution.py:140
  12.1 1.4 %collective-permute-done.2 = bf16[1,72,128]{2,1,0:T(8,128)(2,1)S(1)} collective-permute-done((bf16[1,72,128]{2,1,0:T(8,128)(2,1)S(1)}, bf16[1,72,128]{2,1,0:T(8,128)(2,1)S(1)}, u32[]{:S(2)}, u32[]{:S(2)}) %collective-permute-start.2) | collective-permute-done | bytes 18464 | tf_op jit(solution)/shard_map/ppermute | solution.py:140
  13.6 0.0 collective-permute-done.3
  13.7 1.6 %collective-permute-start.4 = (bf16[10,72,128]{2,1,0:T(8,128)(2,1)S(1)}, bf16[10,72,128]{2,1,0:T(8,128)(2,1)S(1)}, u32[]{:S(2)}, u32[]{:S(2)}) collective-permute-start(bf16[10,72,128]{2,1,0:T(8,128)(2,1)S(1)} %pad_maximum_fusion), channel_id=1, source_target_pairs={{0,1},{1,0},{2,3},{3,2},{4,5},{5,4},{6,7},{7,6},{8,9},{9,8},{10,11... | collective-permute-start | bytes 552968 | tf_op jit(solution)/shard_map/ppermute | solution.py:140
  15.2 0.8 %reshape.12 = f32[3,9,3,3]{1,0,3,2:T(4,128)S(1)} reshape(f32[27,3,3]{0,2,1:T(4,128)} %param.7) | data formatting | bytes 1944 | tf_op jit(solution)/shard_map/reshape | solution.py:183
  16.0 0.1 reshape.13
  16.1 0.1 copy.7.table_ref
  16.2 1.0 %weights.1.weights_ref = bf16[9,96,128]{2,1,0:T(8,128)(2,1)S(1)} custom-call(f32[27,9]{1,0:T(8,128)S(1)} %copy.7.table_ref), custom_call_target="tpu_custom_call" | custom-call | tf_op jit(solution)/shard_map/weights/pallas_call | solution.py:184
  17.2 3.4 %collective-permute-done.4 = bf16[10,72,128]{2,1,0:T(8,128)(2,1)S(1)} collective-permute-done((bf16[10,72,128]{2,1,0:T(8,128)(2,1)S(1)}, bf16[10,72,128]{2,1,0:T(8,128)(2,1)S(1)}, u32[]{:S(2)}, u32[]{:S(2)}) %collective-permute-start.4) | collective-permute-done | bytes 184352 | tf_op jit(solution)/shard_map/ppermute | solution.py:140
  20.7 2.9 %blocks.1 = f32[3456,128]{1,0:T(8,128)} custom-call(bf16[9,96,128]{2,1,0:T(8,128)(2,1)S(1)} %weights.1.weights_ref, bf16[2,10,72,128]{3,2,1,0:T(8,128)(2,1)S(1)} %maximum_select_fusion.field_ref), custom_call_target="tpu_custom_call" | custom-call | tf_op jit(solution)/shard_map/blocks/pallas_call | solution.py:194
  (10 shorter events, 0.2 us)
Async XLA Ops:
  0.0 0.9 %copy-start = (bf16[8,4,4,3,128]{4,2,3,1,0:T(4,128)(2,1)S(1)}, bf16[8,4,4,3,128]{4,2,3,1,0:T(4,128)(2,1)}, u32[]{:S(2)}) copy-start(bf16[8,4,4,3,128]{4,2,3,1,0:T(4,128)(2,1)} %param.4) | copy-start | bytes 294916
  0.9 0.7 %copy-start.1 = (s32[8,4,4]{0,2,1:T(4,128)S(1)}, s32[8,4,4]{0,2,1:T(4,128)}, u32[]{:S(2)}) copy-start(s32[8,4,4]{0,2,1:T(4,128)} %param.5) | copy-start | bytes 1540
  1.6 0.7 %copy-start.2 = (f32[16]{0:T(128)S(1)}, f32[16]{0:T(128)}, u32[]{:S(2)}) copy-start(f32[16]{0:T(128)} %moduli_ref.1) | copy-start | bytes 196
  3.0 7.1 %collective-permute-start = (bf16[8,12,128]{2,1,0:T(8,128)(2,1)S(1)}, bf16[8,12,128]{2,1,0:T(8,128)(2,1)S(1)}, u32[]{:S(2)}, u32[]{:S(2)}) collective-permute-start(bf16[8,12,128]{2,1,0:T(8,128)(2,1)S(1)} %get-tuple-element.7), channel_id=1, source_target_pairs={{0,2},{2,4},{4,6},{6,0},{1,3},{3,5},{5,7},{7,1},{8,10},{10,12},{12... | collective-permute-start | bytes 73736 | tf_op jit(solution)/shard_map/ppermute | solution.py:140
  6.1 4.3 %collective-permute-start.1 = (bf16[8,12,128]{2,1,0:T(8,128)(2,1)S(1)}, bf16[8,12,128]{2,1,0:T(8,128)(2,1)S(1)}, u32[]{:S(2)}, u32[]{:S(2)}) collective-permute-start(bf16[8,12,128]{2,1,0:T(8,128)(2,1)S(1)} %get-tuple-element.8), channel_id=1, source_target_pairs={{0,6},{2,0},{4,2},{6,4},{1,7},{3,1},{5,3},{7,5},{8,14},{10,8},{12,... | collective-permute-start | bytes 73736 | tf_op jit(solution)/shard_map/ppermute | solution.py:140
  10.3 3.2 %collective-permute-start.2 = (bf16[1,72,128]{2,1,0:T(8,128)(2,1)S(1)}, bf16[1,72,128]{2,1,0:T(8,128)(2,1)S(1)}, u32[]{:S(2)}, u32[]{:S(2)}) collective-permute-start(bf16[1,72,128]{2,1,0:T(8,128)(2,1)S(1)} %get-tuple-element.5), channel_id=1, source_target_pairs={{0,8},{8,16},{16,24},{24,0},{1,9},{9,17},{17,25},{25,1},{2,10},{10... | collective-permute-start | bytes 55304 | tf_op jit(solution)/shard_map/ppermute | solution.py:140
  10.4 3.2 %collective-permute-start.3 = (bf16[1,72,128]{2,1,0:T(8,128)(2,1)S(1)}, bf16[1,72,128]{2,1,0:T(8,128)(2,1)S(1)}, u32[]{:S(2)}, u32[]{:S(2)}) collective-permute-start(bf16[1,72,128]{2,1,0:T(8,128)(2,1)S(1)} %get-tuple-element.6), channel_id=1, source_target_pairs={{0,24},{8,0},{16,8},{24,16},{1,25},{9,1},{17,9},{25,17},{2,26},{10... | collective-permute-start | bytes 55304 | tf_op jit(solution)/shard_map/ppermute | solution.py:140
  13.7 7.0 %collective-permute-start.4 = (bf16[10,72,128]{2,1,0:T(8,128)(2,1)S(1)}, bf16[10,72,128]{2,1,0:T(8,128)(2,1)S(1)}, u32[]{:S(2)}, u32[]{:S(2)}) collective-permute-start(bf16[10,72,128]{2,1,0:T(8,128)(2,1)S(1)} %pad_maximum_fusion), channel_id=1, source_target_pairs={{0,1},{1,0},{2,3},{3,2},{4,5},{5,4},{6,7},{7,6},{8,9},{9,8},{10,11... | collective-permute-start | bytes 552968 | tf_op jit(solution)/shard_map/ppermute | solution.py:140
where the time goes:
time: 23.8 us; the launch traced here: 23.5 us
  starting transfers between devices  8.56 us (36%)
  waiting for transfers between devices  7.02 us (29%)
  Pallas kernels  4.51 us (19%)
  local copies, waits for them, and re-layouts  3.22 us (14%)
    ppermute x5, starting transfers between devices, cyclic(): lax.ppermute(array, axis, [(i, (i + step) % peers) for i in range(peers)])  8.56 us
    ppermute x5, waiting for transfers between devices, cyclic(): lax.ppermute(array, axis, [(i, (i + step) % peers) for i in range(peers)])  7.02 us
    pallas_call x1, Pallas kernels, body(): pl.pallas_call(functools.partial(block_kernel, sizes), out_shape=jax.Shap...  2.87 us
    unnamed x6, local copies, waits for them, and re-layouts  2.24 us
    pallas_call x1, Pallas kernels, body(): pl.pallas_call(functools.partial(weight_kernel, cells_y, cells_z), out_sh...  0.96 us
    reshape x2, local copies, waits for them, and re-layouts, body(): stencil.reshape(3, 9, 3, 3)  0.78 us
    pallas_call x1, Pallas kernels, body(): pl.pallas_call(functools.partial(scale_kernel, moduli.shape[0]), out_shap...  0.67 us
  transfers between devices with their start and end apart: 5, of which 4 were waited for; matrix products, arithmetic and copies ran while one was open for 4% of the time, Pallas kernels for 4%

commit v1 on v0

v1 whole, which is shorter than its diff:
```python
import functools

import jax
import jax.numpy as jnp
from jax import lax
from jax.experimental import pallas as pl
from jax.experimental.pallas import tpu as pltpu
from jax.sharding import PartitionSpec as P


VMEM = pltpu.VMEM
LANES = 128


def scale_kernel(moduli_hbm, material_hbm, vectors_hbm, out_ref, moduli_ref, material_ref, vectors_ref, sems):
    copies = [
        pltpu.make_async_copy(source, target, sems.at[i])
        for i, (source, target) in enumerate(
            ((moduli_hbm, moduli_ref), (material_hbm, material_ref), (vectors_hbm, vectors_ref))
        )
    ]
    for copy in copies:
        copy.start()
    copies[0].wait()
    copies[1].wait()
    classes = moduli_ref.shape[0]
    cells_y, cells_z, cells_x = material_ref.shape
    parts = vectors_ref.shape[2]
    roots = []
    for y in range(cells_y):
        material = material_ref[y]
        modulus = jnp.zeros(material.shape, jnp.float32)
        for c in range(classes):
            modulus = jnp.where(material == c, moduli_ref[c], modulus)
        roots.append(jnp.sqrt(modulus))
    copies[2].wait()
    for x in range(cells_x):
        for y in range(cells_y):
            factor = jnp.broadcast_to(roots[y][:, x : x + 1], (cells_z, vectors_ref.shape[-1]))
            for a in range(parts):
                row = (y * parts + a) * cells_z
                value = vectors_ref[x, y, a].astype(jnp.float32) * factor
                out_ref[x, row : row + cells_z, :] = value.astype(jnp.bfloat16)


def weight_kernel(cells_z, stencil_hbm, out_ref, stencil_ref, sem):
    copy = pltpu.make_async_copy(stencil_hbm, stencil_ref, sem)
    copy.start()
    _, rows, lanes = out_ref.shape
    parts, _, neighbours = stencil_ref.shape
    half = rows // 2
    block = parts * cells_z
    cells_y = half // block
    row = lax.broadcasted_iota(jnp.int32, (half, lanes), 0)
    lane = lax.broadcasted_iota(jnp.int32, (half, lanes), 1)
    slot = lane // block
    lane_y = jnp.where(slot < cells_y, slot, jnp.where(slot == cells_y, -1, cells_y))
    shift_y = jnp.where(slot < cells_y + 2, lane_y - row // block, 9)
    shift_z = lane % cells_z - row % cells_z
    pick_row = lax.broadcasted_iota(jnp.int32, (half, parts * neighbours), 0)
    pick_col = lax.broadcasted_iota(jnp.int32, (half, parts * neighbours), 1)
    pick_col = pick_col - neighbours * ((pick_row % block) // cells_z)
    spread = lax.broadcasted_iota(jnp.int32, (parts, lanes), 0) == (
        (lax.broadcasted_iota(jnp.int32, (parts, lanes), 1) % block) // cells_z
    )
    spread = spread.astype(jnp.float32).astype(jnp.bfloat16)
    wide = []
    copy.wait()
    for a in range(parts):
        exact = stencil_ref[a]
        high = exact.astype(jnp.bfloat16)
        low = (exact - high.astype(jnp.float32)).astype(jnp.bfloat16)
        wide.append(
            [
                lax.dot_general(piece, spread, (((0,), (0,)), ((), ())), preferred_element_type=jnp.float32)
                for piece in (high, low)
            ]
        )
    wide = [jnp.concatenate([w[h] for w in wide], axis=0).astype(jnp.bfloat16) for h in range(2)]
    wide = jnp.concatenate(wide, axis=1)
    for k in range(3):
        totals = [[jnp.zeros((half, lanes), jnp.float32) for _ in range(2)] for _ in range(3)]
        for dy in range(3):
            for dz in range(3):
                pick = (pick_col == 9 * k + 3 * dy + dz).astype(jnp.float32).astype(jnp.bfloat16)
                value = jnp.dot(pick, wide, preferred_element_type=jnp.float32)
                for oz in range(3):
                    here = (shift_y == dy - 1) & (shift_z == dz - 1 - (oz - 1) * cells_z)
                    for h in range(2):
                        totals[oz][h] = jnp.where(here, value[:, h * lanes : (h + 1) * lanes], totals[oz][h])
        for oz in range(3):
            for h in range(2):
                out_ref[3 * k + oz, h * half : (h + 1) * half, :] = totals[oz][h].astype(jnp.bfloat16)


def block_kernel(share, places, weights_ref, *refs):
    owners = len(places(0))
    cells, rims, faces = refs[0:owners], refs[owners : 2 * owners], refs[2 * owners : 3 * owners]
    out_ref, turned_ref, image_ref = refs[3 * owners :]
    cells_x, own_rows, width = cells[0].shape
    rim_rows = rims[0].shape[1]
    rows = own_rows + rim_rows
    me = lax.axis_index("gz")
    place = places(me)
    first = me * share
    lane = lax.broadcasted_iota(jnp.int32, (share, LANES), 1)
    masks = [
        (lane >= own_rows) & (lane < own_rows + rim_rows // 2),
        lane < own_rows,
        (lane >= own_rows + rim_rows // 2) & (lane < rows),
    ]
    pad = jnp.zeros((LANES - rows, width), jnp.bfloat16)
    stride = 27 * owners

    def plane(v, x):
        if x < cells_x:
            return jnp.concatenate([cells[v][x], rims[v][x], pad], axis=0)
        return jnp.concatenate([faces[v][x - cells_x], pad], axis=0)

    def put(n, u, value):
        out_ref[pl.ds(n * owners + place[u], share, stride=stride), :] = value

    for u in range(owners):
        for x in range(cells_x):
            own = cells[u][x]
            turned_ref[...] = jnp.concatenate([own, own], axis=0).T
            image_ref[x * share : (x + 1) * share, :] = turned_ref[pl.ds(first, share), :]
        lhs = image_ref[...]
        if owners == 2:
            toward = place[1 - u] - place[u] + 1
            near, missing = [(u, 1), (1 - u, toward)], [2 - toward]
        else:
            near = [(v, v - u + 1) for v in range(max(u - 1, 0), min(u + 2, owners))]
            missing = [oz for oz in range(3) if not 0 <= u + oz - 1 < owners]
        for oz in missing:
            zero = jnp.zeros((share, width), jnp.float32)
            for n in range(0, 27, 3):
                put(n + oz, u, zero)
        for v, oz in near:
            products = [
                jnp.dot(lhs, weights_ref[3 * k + oz], preferred_element_type=jnp.float32) for k in range(3)
            ]

            def image(x):
                total = None
                for k in range(3):
                    source = x - (k - 1)
                    if 0 <= source < cells_x:
                        term = products[k][source * share : (source + 1) * share, :]
                        total = term if total is None else total + term
                return jnp.concatenate(
                    [jnp.where(mask, total, 0.0).astype(jnp.bfloat16) for mask in masks], axis=0
                )

            middle = None
            for x in range(0, cells_x, 2):
                left = jnp.concatenate([image(x), image(x + 1)], axis=1)
                right = jnp.concatenate([plane(v, x), plane(v, x + 1)], axis=0)
                term = jnp.dot(left, right, preferred_element_type=jnp.float32)
                middle = term if middle is None else middle + term
            before = jnp.dot(image(-1), plane(v, cells_x), preferred_element_type=jnp.float32)
            after = jnp.dot(image(cells_x), plane(v, cells_x + 1), preferred_element_type=jnp.float32)
            for ox, value in enumerate((before, middle, after)):
                for oy in range(3):
                    put(9 * ox + 3 * oy + oz, u, value[oy * share : (oy + 1) * share, :])


def in_hbm(array):
    return pltpu.with_memory_space_constraint(array, pltpu.HBM)


def cyclic(array, axis, step):
    peers = lax.axis_size(axis)
    return lax.ppermute(array, axis, [(i, (i + step) % peers) for i in range(peers)])


def halo(first, last, axis):
    peers, place = lax.axis_size(axis), lax.axis_index(axis)
    before = cyclic(last, axis, 1)
    after = cyclic(first, axis, -1)
    zero = jnp.zeros_like(before)
    return jnp.where(place == 0, zero, before), jnp.where(place == peers - 1, zero, after)


def columns(first, last):
    wide, peers = lax.axis_size("gx"), lax.axis_size("gy")
    if wide % 2:
        return halo(first, last, "gy")

    def target(p, q):
        if p % 2 == 0:
            return (p, q + 1) if q + 1 < peers else (p + 1, q)
        return (p, q - 1) if q > 0 else (p - 1, q)

    pairs = []
    for p in range(wide):
        for q in range(peers):
            to_p, to_q = target(p, q)
            pairs.append((p * peers + q, to_p * peers + to_q))
    place = lax.axis_index("gy")
    odd = lax.axis_index("gx") % 2 == 1
    ahead = lax.ppermute(jnp.where(odd, first, last), ("gx", "gy"), pairs)
    back = lax.ppermute(jnp.where(odd, last, first), ("gx", "gy"), [(t, f) for f, t in pairs])
    zero = jnp.zeros_like(ahead)
    before, after = jnp.where(odd, back, ahead), jnp.where(odd, ahead, back)
    return jnp.where(place == 0, zero, before), jnp.where(place == peers - 1, zero, after)


def line(array):
    owners = lax.axis_size("gz")
    if owners == 2:
        return [array, cyclic(array, "gz", 1)]
    gathered = lax.all_gather(array, "gz")
    return [gathered[v] for v in range(owners)]


def blocks(deflation, material, moduli, stencil):
    cells_x, cells_y, cells_z, parts, width = deflation.shape
    owners = lax.axis_size("gz")
    share = width // owners
    side = parts * cells_z
    own_rows = cells_y * side
    small = pltpu.CompilerParams(vmem_limit_bytes=16 << 20)
    vectors = jnp.transpose(deflation, (0, 1, 3, 2, 4))
    classes = jnp.transpose(material, (1, 2, 0))

    scaled = pl.pallas_call(
        scale_kernel,
        out_shape=jax.ShapeDtypeStruct((cells_x, own_rows, width), jnp.bfloat16),
        in_specs=[pl.BlockSpec(memory_space=pltpu.HBM)] * 3,
        out_specs=pl.BlockSpec(memory_space=VMEM),
        scratch_shapes=[
            pltpu.SMEM(moduli.shape, moduli.dtype),
            VMEM(classes.shape, classes.dtype),
            VMEM(vectors.shape, vectors.dtype),
            pltpu.SemaphoreType.DMA((3,)),
        ],
        compiler_params=small,
        name="scale",
    )(*(in_hbm(v) for v in (moduli, classes, vectors)))

    coupling = jnp.transpose(stencil, (1, 2, 0))
    weights = pl.pallas_call(
        functools.partial(weight_kernel, cells_z),
        out_shape=jax.ShapeDtypeStruct((9, 2 * own_rows, LANES), jnp.bfloat16),
        in_specs=[pl.BlockSpec(memory_space=pltpu.HBM)],
        out_specs=pl.BlockSpec(memory_space=VMEM),
        scratch_shapes=[VMEM(coupling.shape, coupling.dtype), pltpu.SemaphoreType.DMA],
        compiler_params=small,
        name="weights",
    )(in_hbm(coupling))

    before, after = columns(scaled[:, :side], scaled[:, own_rows - side :])
    cells = line(scaled)
    rim = jnp.concatenate([before, after], axis=1)
    rims = line(rim)
    first = jnp.concatenate([scaled[0], rim[0]], axis=0)
    last = jnp.concatenate([scaled[cells_x - 1], rim[cells_x - 1]], axis=0)
    left, right = halo(first, last, "gx")
    faces = line(jnp.stack([left, right]))

    def places(me):
        return [me, 1 - me] if owners == 2 else list(range(owners))

    coarse = pl.pallas_call(
        functools.partial(block_kernel, share, places),
        out_shape=jax.ShapeDtypeStruct((share * 27 * owners, width), jnp.float32),
        in_specs=[pl.BlockSpec(memory_space=VMEM)] * (1 + 3 * owners),
        out_specs=pl.BlockSpec(memory_space=VMEM),
        scratch_shapes=[
            VMEM((width, 2 * own_rows), jnp.bfloat16),
            VMEM((cells_x * share, 2 * own_rows), jnp.bfloat16),
        ],
        compiler_params=pltpu.CompilerParams(vmem_limit_bytes=32 << 20),
        name="blocks",
    )(weights, *cells, *rims, *faces)
    coarse = coarse.reshape(share, 27, owners, width)
    return jnp.transpose(coarse, (0, 2, 1, 3)).reshape(1, 1, share, owners, 27, width)


def solution(mesh):
    in_specs = (P("gx", "gy", "gz", None, None), P("gx", "gy", "gz"), P(), P())
    out_specs = P("gx", "gy", "gz", None, None, None)
    return jax.shard_map(blocks, mesh=mesh, in_specs=in_specs, out_specs=out_specs, check_vma=False)
```

time: 23.8 us -> 19.8 us (0.83)
  local copies, waits for them, and re-layouts: 3.22 us -> 0.01 us
  starting transfers between devices: 8.56 us -> 7.31 us
  Pallas kernels: 4.51 us -> 5.15 us
    ppermute x5, starting transfers between devices: 8.56 us -> 5.28 us  [cyclic(): lax.ppermute(array, axis, [(i, (i + step) % peers) for i in range(peers)])]
    unnamed x6 -> x0, local copies, waits for them, and re-layouts: 2.24 us -> none
    ppermute x5, waiting for transfers between devices: 7.02 us -> 4.87 us  [cyclic(): lax.ppermute(array, axis, [(i, (i + step) % peers) for i in range(peers)])]
    ppermute x0 -> x2, waiting for transfers between devices: none -> 2.12 us  [the longest x1 2.12 us: columns(): lax.ppermute(jnp.where(odd, last, first), ('gx', 'gy'), [(t, f) for f, t...]
    ppermute x0 -> x2, starting transfers between devices: none -> 2.03 us  [the longest x1 2.01 us: columns(): ahead = lax.ppermute(jnp.where(odd, first, last), ('gx', 'gy'), pairs)]
    reshape x4 -> x0, local copies, waits for them, and re-layouts: 0.96 us -> none  [the longest x2 0.78 us: body(): stencil.reshape(3, 9, 3, 3)]
    pallas_call x3, Pallas kernels: 4.51 us -> 5.15 us  [the longest x1 2.86 us: blocks(): pl.pallas_call(functools.partial(block_kernel, share, places), out_shape=...]
  transfers between devices with their start and end apart: 5 -> 7, of which waited for: 4 -> 4; matrix products, arithmetic and copies ran while one was open for 4% -> 0% of each run, Pallas kernels for 4% -> 6%
where the time goes in v1:
time: 19.8 us; the launch traced here: 19.6 us
  starting transfers between devices  7.31 us (37%)
  waiting for transfers between devices  6.99 us (35%)
  Pallas kernels  5.15 us (26%)
    ppermute x5, starting transfers between devices, cyclic(): lax.ppermute(array, axis, [(i, (i + step) % peers) for i in range(peers)])  5.28 us
    ppermute x5, waiting for transfers between devices, cyclic(): lax.ppermute(array, axis, [(i, (i + step) % peers) for i in range(peers)])  4.87 us
    pallas_call x1, Pallas kernels, blocks(): pl.pallas_call(functools.partial(block_kernel, share, places), out_shape=...  2.86 us
    ppermute x1, waiting for transfers between devices, columns(): lax.ppermute(jnp.where(odd, last, first), ('gx', 'gy'), [(t, f) for f, t...  2.12 us
    ppermute x1, starting transfers between devices, columns(): ahead = lax.ppermute(jnp.where(odd, first, last), ('gx', 'gy'), pairs)  2.01 us
    pallas_call x1, Pallas kernels, blocks(): pl.pallas_call(functools.partial(weight_kernel, cells_z), out_shape=jax.S...  1.24 us
    pallas_call x1, Pallas kernels, blocks(): pl.pallas_call(scale_kernel, out_shape=jax.ShapeDtypeStruct((cells_x, own...  1.05 us
  transfers between devices with their start and end apart: 7, of which 4 were waited for; matrix products, arithmetic and copies ran while one was open for 0% of the time, Pallas kernels for 6%

profile of v1, /device:TPU:0, one launch (start us, length us, event | category | flops | bytes accessed | tf_op | source)
XLA Modules:
  0.0 19.6 jit_solution(17074692639417894904)
XLA Ops:
  0.0 1.0 %scale.1.refs_0_ = bf16[8,48,128]{2,1,0:T(8,128)(2,1)S(1)} custom-call(f32[16]{0:T(128)} %moduli_hbm.1, s32[4,4,8]{2,1,0:T(4,128)} %bitcast.21, bf16[8,4,3,4,128]{4,3,2,1,0:T(4,128)(2,1)} %bitcast.20), custom_call_target="tpu_custom_call" | custom-call | tf_op jit(solution)/shard_map/scale/pallas_call | solution.py:227
  1.1 3.1 %collective-permute-start = (bf16[8,48,128]{2,1,0:T(8,128)(2,1)S(1)}, bf16[8,48,128]{2,1,0:T(8,128)(2,1)S(1)}, u32[]{:S(2)}, u32[]{:S(2)}) collective-permute-start(bf16[8,48,128]{2,1,0:T(8,128)(2,1)S(1)} %scale.1.refs_0_), channel_id=1, source_target_pairs={{0,1},{1,0},{2,3},{3,2},{4,5},{5,4},{6,7},{7,6},{8,9},{9,8},{10,11... | collective-permute-start | bytes 294920 | tf_op jit(solution)/shard_map/ppermute | solution.py:174
  4.1 0.0 collective-permute-start.1
  4.2 2.0 %collective-permute-start.2 = (bf16[8,12,128]{2,1,0:T(8,128)(2,1)S(1)}, bf16[8,12,128]{2,1,0:T(8,128)(2,1)S(1)}, u32[]{:S(2)}, u32[]{:S(2)}) collective-permute-start(bf16[8,12,128]{2,1,0:T(8,128)(2,1)S(1)} %get-tuple-element.8), channel_id=1, source_target_pairs={{0,2},{2,4},{4,6},{6,14},{8,0},{10,8},{12,10},{14,12},{16,18},{18,... | collective-permute-start | bytes 73736 | tf_op jit(solution)/shard_map/ppermute | solution.py:202
  6.2 2.1 %collective-permute-done.1 = bf16[8,12,128]{2,1,0:T(8,128)(2,1)S(1)} collective-permute-done((bf16[8,12,128]{2,1,0:T(8,128)(2,1)S(1)}, bf16[8,12,128]{2,1,0:T(8,128)(2,1)S(1)}, u32[]{:S(2)}, u32[]{:S(2)}) %collective-permute-start.1) | collective-permute-done | bytes 24608 | tf_op jit(solution)/shard_map/ppermute | solution.py:203
  8.3 0.0 collective-permute-done.2
  8.4 1.1 %collective-permute-start.5 = (bf16[72,128]{1,0:T(8,128)(2,1)S(1)}, bf16[72,128]{1,0:T(8,128)(2,1)S(1)}, u32[]{:S(2)}, u32[]{:S(2)}) collective-permute-start(bf16[72,128]{1,0:T(8,128)(2,1)S(1)} %pad_maximum_fusion.3), channel_id=1, source_target_pairs={{0,24},{8,0},{16,8},{24,16},{1,25},{9,1},{17,9},{25,17},{2,26},{10... | collective-permute-start | bytes 55304 | tf_op jit(solution)/shard_map/ppermute | solution.py:174
  9.5 0.0 collective-permute-start.4
  9.5 0.5 %collective-permute-start.3 = (bf16[8,24,128]{2,1,0:T(8,128)(2,1)S(1)}, bf16[8,24,128]{2,1,0:T(8,128)(2,1)S(1)}, u32[]{:S(2)}, u32[]{:S(2)}) collective-permute-start(bf16[8,24,128]{2,1,0:T(8,128)(2,1)S(1)} %pad_maximum_fusion.refs_2_), channel_id=1, source_target_pairs={{0,1},{1,0},{2,3},{3,2},{4,5},{5,4},{6,7},{7,6},{8,9},{9,8},{10,11... | collective-permute-start | bytes 147464 | tf_op jit(solution)/shard_map/ppermute | solution.py:174
  10.0 1.0 %collective-permute-done.5 = bf16[72,128]{1,0:T(8,128)(2,1)S(1)} collective-permute-done((bf16[72,128]{1,0:T(8,128)(2,1)S(1)}, bf16[72,128]{1,0:T(8,128)(2,1)S(1)}, u32[]{:S(2)}, u32[]{:S(2)}) %collective-permute-start.5) | collective-permute-done | bytes 18464 | tf_op jit(solution)/shard_map/ppermute | solution.py:174
  11.0 1.7 %collective-permute-done.4 = bf16[72,128]{1,0:T(8,128)(2,1)S(1)} collective-permute-done((bf16[72,128]{1,0:T(8,128)(2,1)S(1)}, bf16[72,128]{1,0:T(8,128)(2,1)S(1)}, u32[]{:S(2)}, u32[]{:S(2)}) %collective-permute-start.4) | collective-permute-done | bytes 18464 | tf_op jit(solution)/shard_map/ppermute | solution.py:174
  12.7 0.6 %collective-permute-start.6 = (bf16[2,72,128]{2,1,0:T(8,128)(2,1)S(1)}, bf16[2,72,128]{2,1,0:T(8,128)(2,1)S(1)}, u32[]{:S(2)}, u32[]{:S(2)}) collective-permute-start(bf16[2,72,128]{2,1,0:T(8,128)(2,1)S(1)} %pad_maximum_fusion.1.refs_4_), channel_id=1, source_target_pairs={{0,1},{1,0},{2,3},{3,2},{4,5},{5,4},{6,7},{7,6},{8,9},{9,8},{10,11... | collective-permute-start | bytes 110600 | tf_op jit(solution)/shard_map/ppermute | solution.py:174
  13.3 1.2 %weights.1.weights_ref = bf16[9,96,128]{2,1,0:T(8,128)(2,1)S(1)} custom-call(f32[3,3,27]{2,1,0:T(4,128)} %bitcast.22), custom_call_target="tpu_custom_call" | custom-call | tf_op jit(solution)/shard_map/weights/pallas_call | solution.py:243
  14.5 0.0 collective-permute-done.3.refs_3_
  14.6 2.2 %collective-permute-done.6.refs_5_ = bf16[2,72,128]{2,1,0:T(8,128)(2,1)S(1)} collective-permute-done((bf16[2,72,128]{2,1,0:T(8,128)(2,1)S(1)}, bf16[2,72,128]{2,1,0:T(8,128)(2,1)S(1)}, u32[]{:S(2)}, u32[]{:S(2)}) %collective-permute-start.6) | collective-permute-done | bytes 36896 | tf_op jit(solution)/shard_map/ppermute | solution.py:174
  16.8 0.0 collective-permute-done.refs_1_
  16.8 2.9 %blocks.1 = f32[3456,128]{1,0:T(8,128)} custom-call(bf16[9,96,128]{2,1,0:T(8,128)(2,1)S(1)} %weights.1.weights_ref, bf16[8,48,128]{2,1,0:T(8,128)(2,1)S(1)} %scale.1.refs_0_, bf16[8,48,128]{2,1,0:T(8,128)(2,1)S(1)} %collective-permute-done.refs_1_, bf16[8,24,128]{2,1,0:T(8,128)(2,1)S(1)} %pad_maximum_fusion.refs_2_, ...), custom_call_target="tpu_custom_call" | custom-call | tf_op jit(solution)/shard_map/blocks/pallas_call | solution.py:265
  (10 shorter events, 0.1 us)
Async XLA Ops:
  1.1 15.7 %collective-permute-start = (bf16[8,48,128]{2,1,0:T(8,128)(2,1)S(1)}, bf16[8,48,128]{2,1,0:T(8,128)(2,1)S(1)}, u32[]{:S(2)}, u32[]{:S(2)}) collective-permute-start(bf16[8,48,128]{2,1,0:T(8,128)(2,1)S(1)} %scale.1.refs_0_), channel_id=1, source_target_pairs={{0,1},{1,0},{2,3},{3,2},{4,5},{5,4},{6,7},{7,6},{8,9},{9,8},{10,11... | collective-permute-start | bytes 294920 | tf_op jit(solution)/shard_map/ppermute | solution.py:174
  4.1 4.2 %collective-permute-start.1 = (bf16[8,12,128]{2,1,0:T(8,128)(2,1)S(1)}, bf16[8,12,128]{2,1,0:T(8,128)(2,1)S(1)}, u32[]{:S(2)}, u32[]{:S(2)}) collective-permute-start(bf16[8,12,128]{2,1,0:T(8,128)(2,1)S(1)} %get-tuple-element.7), channel_id=1, source_target_pairs={{2,0},{4,2},{6,4},{14,6},{0,8},{8,10},{10,12},{12,14},{18,16},{20,... | collective-permute-start | bytes 73736 | tf_op jit(solution)/shard_map/ppermute | solution.py:203
  4.2 4.1 %collective-permute-start.2 = (bf16[8,12,128]{2,1,0:T(8,128)(2,1)S(1)}, bf16[8,12,128]{2,1,0:T(8,128)(2,1)S(1)}, u32[]{:S(2)}, u32[]{:S(2)}) collective-permute-start(bf16[8,12,128]{2,1,0:T(8,128)(2,1)S(1)} %get-tuple-element.8), channel_id=1, source_target_pairs={{0,2},{2,4},{4,6},{6,14},{8,0},{10,8},{12,10},{14,12},{16,18},{18,... | collective-permute-start | bytes 73736 | tf_op jit(solution)/shard_map/ppermute | solution.py:202
  8.4 2.6 %collective-permute-start.5 = (bf16[72,128]{1,0:T(8,128)(2,1)S(1)}, bf16[72,128]{1,0:T(8,128)(2,1)S(1)}, u32[]{:S(2)}, u32[]{:S(2)}) collective-permute-start(bf16[72,128]{1,0:T(8,128)(2,1)S(1)} %pad_maximum_fusion.3), channel_id=1, source_target_pairs={{0,24},{8,0},{16,8},{24,16},{1,25},{9,1},{17,9},{25,17},{2,26},{10... | collective-permute-start | bytes 55304 | tf_op jit(solution)/shard_map/ppermute | solution.py:174
  9.5 3.2 %collective-permute-start.4 = (bf16[72,128]{1,0:T(8,128)(2,1)S(1)}, bf16[72,128]{1,0:T(8,128)(2,1)S(1)}, u32[]{:S(2)}, u32[]{:S(2)}) collective-permute-start(bf16[72,128]{1,0:T(8,128)(2,1)S(1)} %pad_maximum_fusion.2), channel_id=1, source_target_pairs={{0,8},{8,16},{16,24},{24,0},{1,9},{9,17},{17,25},{25,1},{2,10},{10... | collective-permute-start | bytes 55304 | tf_op jit(solution)/shard_map/ppermute | solution.py:174
  9.5 5.0 %collective-permute-start.3 = (bf16[8,24,128]{2,1,0:T(8,128)(2,1)S(1)}, bf16[8,24,128]{2,1,0:T(8,128)(2,1)S(1)}, u32[]{:S(2)}, u32[]{:S(2)}) collective-permute-start(bf16[8,24,128]{2,1,0:T(8,128)(2,1)S(1)} %pad_maximum_fusion.refs_2_), channel_id=1, source_target_pairs={{0,1},{1,0},{2,3},{3,2},{4,5},{5,4},{6,7},{7,6},{8,9},{9,8},{10,11... | collective-permute-start | bytes 147464 | tf_op jit(solution)/shard_map/ppermute | solution.py:174
  12.7 4.0 %collective-permute-start.6 = (bf16[2,72,128]{2,1,0:T(8,128)(2,1)S(1)}, bf16[2,72,128]{2,1,0:T(8,128)(2,1)S(1)}, u32[]{:S(2)}, u32[]{:S(2)}) collective-permute-start(bf16[2,72,128]{2,1,0:T(8,128)(2,1)S(1)} %pad_maximum_fusion.1.refs_4_), channel_id=1, source_target_pairs={{0,1},{1,0},{2,3},{3,2},{4,5},{5,4},{6,7},{7,6},{8,9},{9,8},{10,11... | collective-permute-start | bytes 110600 | tf_op jit(solution)/shard_map/ppermute | solution.py:174
